TPU v7x, 32 devices: a whole 2x2x4 slice. The times are simulated.
32 devices in a mesh: ga: 8 (over y, x, core), ba: 4 (over z).
Axes of the slice: x: 2, y: 2, z: 4, core: 2. Of those that a mesh axis runs over, the one named last changes fastest.
Arguments:
- psi: float32 [2, 16384, 2048], P(None, 'ga', 'ba'), may hold values from -0.1875 to 0.1875
- dpsi: float32 [2, 16384, 512], P(None, 'ga', 'ba'), may hold values from -6 to 6
- band_weight: float32 [2048], replicated, may hold values from 0.25 to 1
- panel_band: int32 [16], P('ba'), may hold values from 0 to 15, each once
- slab_offset: int32 [8], replicated, may hold values from 0 to 2047
Outputs:
- projected: float32 [2, 16384, 512], P(None, 'ga', 'ba')
Inputs may be any that keep to these rules, and one draw needn't show every extreme that they name: panel_band is a permutation of the panel numbers.
All inputs are finite; a program needn't handle non-finite values.
Results may differ from a plain program's by a relative error of at most 0.00012.
Values sent between devices are 32-bit elements; how exact they have to be, the bound alone decides.
A program may use at most 128 MiB of HBM per device.

v0:
```python
import functools
import jax
import jax.numpy as jnp
from jax import lax
from jax.sharding import PartitionSpec as P

PANEL = 128


def tdot(left, right):
    return lax.dot_general(
        left,
        right,
        (((0,), (0,)), ((), ())),
        precision=lax.Precision.HIGH,
        preferred_element_type=jnp.float32,
    )


def mdot(left, right):
    return jnp.dot(left, right, precision=lax.Precision.HIGH, preferred_element_type=jnp.float32)


CHUNKS = 2


def turned(packed, width):
    column = lax.broadcasted_iota(jnp.int32, packed.shape, 1)
    first = column // width % 2 == 0
    return jnp.where(first, jnp.roll(packed, -width, axis=1), -jnp.roll(packed, width, axis=1))


def sum_over(block, axis, size):
    if size & size - 1 or block.shape[0] % size:
        return lax.psum(block, axis)
    place = lax.axis_index(axis)
    bits = [1 << b for b in range(size.bit_length() - 1)]
    for bit in bits:
        upper = place // bit % 2
        half = block.shape[0] // 2
        kept = lax.dynamic_slice_in_dim(block, upper * half, half, 0)
        sent = lax.dynamic_slice_in_dim(block, (1 - upper) * half, half, 0)
        block = kept + lax.ppermute(sent, axis, [(i, i ^ bit) for i in range(size)])
    for bit in reversed(bits):
        upper = place // bit % 2 == 1
        other = lax.ppermute(block, axis, [(i, i ^ bit) for i in range(size)])
        block = jnp.concatenate([jnp.where(upper, other, block), jnp.where(upper, block, other)])
    return block


def weights_for(band_weight, panels):
    table = band_weight.reshape(-1, PANEL)
    onehot = (panels[:, None] == jnp.arange(table.shape[0], dtype=jnp.int32)[None, :]).astype(
        jnp.float32
    )
    return mdot(onehot, table).reshape(-1)


def per_device(size, psi, dpsi, band_weight, panel_band, slab_offset):
    offset = slab_offset[lax.axis_index("ga")]
    aligned = jnp.roll(dpsi, -offset, axis=1)
    local_weight = weights_for(band_weight, panel_band)
    width = aligned.shape[2] // CHUNKS
    pieces = []
    for chunk in range(CHUNKS):
        columns = slice(chunk * width, (chunk + 1) * width)
        own = jnp.concatenate([aligned[0, :, columns], aligned[1, :, columns]], axis=1)
        every = lax.all_gather(own, "ba", axis=1, tiled=True)
        block = tdot(psi[0], every) + turned(tdot(psi[1], every), width)
        weighted = sum_over(block, "ga", size) * local_weight[:, None]
        correction = mdot(psi[0], weighted) - mdot(psi[1], turned(weighted, width))
        share = lax.psum_scatter(correction, "ba", scatter_dimension=1, tiled=True)
        pieces.append(own - share)
    result = jnp.stack(
        [
            jnp.concatenate(
                [piece[:, part * width : (part + 1) * width] for piece in pieces], axis=1
            )
            for part in range(2)
        ]
    )
    return jnp.roll(result, offset, axis=1)


def solution(mesh):
    in_specs = (P(None, "ga", "ba"), P(None, "ga", "ba"), P(), P("ba"), P())
    out_specs = P(None, "ga", "ba")
    return jax.shard_map(
        functools.partial(per_device, mesh.shape["ga"]),
        mesh=mesh,
        in_specs=in_specs,
        out_specs=out_specs,
        check_vma=False,
    )
```

profile of v0, /device:TPU:0, one launch (start us, length us, event | category | flops | bytes accessed | tf_op | source)
XLA Modules:
  0.0 425.5 jit_solution(11217355059980172161)
XLA Ops:
  6.5 1.2 dynamic_slice.42
  8.9 1.9 copy.6
  10.9 1.2 fusion.31
  12.2 1.0 pad_maximum_fusion.1
  13.4 1.0 pad_maximum_fusion
  14.5 82.4 %all-gather.5.cloned.1.call-done = f32[2048,512]{0,1:T(8,128)} async-done(((f32[2048,128]{0,1:T(8,128)}), f32[2048,512]{0,1:T(8,128)}) %all-gather.5.cloned.1.call-update) | async-done | bytes 4194320 | tf_op jit(solution)/shard_map/all_gather | solution.py:68
  96.9 6.5 %fusion.41 = f32[512,512]{1,0:T(8,128)S(1)} fusion(f32[2048,512]{0,1:T(8,128)} %all-gather.5.cloned.1.call-done, f32[2,2048,512]{2,1,0:T(8,128)} %param.7), kind=kOutput, calls=%fused_computation.44 | convolution fusion | flops 3221225472 | bytes 9437184 | tf_op jit(solution)/shard_map/dot_general | solution.py:11
  103.4 0.8 fusion.79
  104.2 1.7 fusion.80
  105.9 71.8 %all-gather.3.cloned.1.call-done = f32[2048,512]{0,1:T(8,128)} async-done(((f32[2048,128]{0,1:T(8,128)}), f32[2048,512]{0,1:T(8,128)}) %all-gather.3.cloned.1.call-update) | async-done | bytes 4194320 | tf_op jit(solution)/shard_map/all_gather | solution.py:68
  177.8 6.7 %fusion.38 = f32[512,512]{1,0:T(8,128)S(1)} fusion(f32[2048,512]{0,1:T(8,128)} %all-gather.3.cloned.1.call-done, f32[2,2048,512]{2,1,0:T(8,128)} %param.7), kind=kOutput, calls=%fused_computation.43 | convolution fusion | flops 3221225472 | bytes 9437184 | tf_op jit(solution)/shard_map/dot_general | solution.py:11
  185.0 0.7 copy-done.4
  185.7 6.3 %fusion.44 = f32[512,512]{1,0:T(8,128)S(1)} fusion(f32[2048,512]{0,1:T(8,128)S(1)} %copy-done.3, f32[2,2048,512]{2,1,0:T(8,128)} %param.7, f32[512,64]{1,0:T(8,128)S(1)} %copy-done.6, f32[512,448]{1,0:T(8,128)S(1)} %copy-done.5, f32[512,448]{1,0:T(8,128)S(1)} %copy-done.4, f32[512,64]{1,0:T(8,128)S(1)} %get-tuple-element.30, ...), kind=kOutput, calls=%fused_computation.45 | convolution fusion | flops 3225944064 | bytes 11538944 | tf_op jit(solution)/shard_map/dot_general | solution.py:11
  192.0 0.8 constant_dynamic-slice_fusion.2
  192.8 4.9 %fusion.47 = f32[512,512]{1,0:T(8,128)} fusion(f32[2048,512]{0,1:T(8,128)S(1)} %copy-done.2, f32[2,2048,512]{2,1,0:T(8,128)S(1)} %bitcast.75, f32[512,64]{1,0:T(8,128)S(1)} %get-tuple-element.21, f32[512,448]{1,0:T(8,128)S(1)} %get-tuple-element.23, f32[512,448]{1,0:T(8,128)S(1)} %get-tuple-element.22, f32[512,64]{1,0:T(8,128)S(1)} %get-tuple-element.20, ...), kind=kOutput, calls=%fused_computation.46 | convolution fusion | flops 3225944064 | bytes 12063232 | tf_op jit(solution)/shard_map/dot_general | solution.py:11
  197.7 1.9 constant_dynamic-slice_fusion.5
  199.6 0.5 collective-permute-start
  200.1 1.2 dynamic-slice_add_fusion
  201.3 1.5 collective-permute-start.7
  202.8 1.3 dynamic-slice_add_fusion.1
  204.1 0.7 collective-permute-start.1
  204.8 5.7 %collective-permute-done.7 = f32[128,512]{1,0:T(8,128)S(1)} collective-permute-done((f32[128,512]{1,0:T(8,128)S(1)}, f32[128,512]{1,0:T(8,128)S(1)}, u32[]{:S(2)}, u32[]{:S(2)}) %collective-permute-start.7) | collective-permute-done | bytes 262176 | tf_op jit(solution)/shard_map/ppermute | solution.py:43
  210.6 1.5 collective-permute-start.8
  212.1 3.1 collective-permute-done.1
  215.2 1.5 collective-permute-start.2
  216.8 0.6 collective-permute-start.9
  217.4 4.2 collective-permute-done.2
  221.6 1.5 collective-permute-start.3
  223.1 1.0 collective-permute-done.9
  224.1 1.5 collective-permute-start.10
  225.6 1.0 collective-permute-done.3
  226.7 1.5 collective-permute-start.4
  228.2 4.0 collective-permute-done.10
  232.3 0.8 pad_maximum_fusion.3
  233.1 1.9 collective-permute-done.4
  235.1 0.8 pad_maximum_fusion.2
  236.1 1.2 broadcast_select_fusion.1
  237.3 0.9 collective-permute-done.5
  238.1 1.2 broadcast_select_fusion.3
  240.1 9.8 %fusion.4 = f32[512,2048]{1,0:T(8,128)S(1)} fusion(f32[2,2048,512]{2,1,0:T(8,128)} %param.7, f32[512,64]{1,0:T(8,128)S(1)} %get-tuple-element.15, f32[512,448]{1,0:T(8,128)S(1)} %get-tuple-element.17, f32[512,448]{1,0:T(8,128)S(1)} %get-tuple-element.16, f32[512,64]{1,0:T(8,128)S(1)} %get-tuple-element.14, s32[512]{0:T(512)S(1)} %iota_shift-right-logical_fusion, ...), kind=kOutput, calls=%fused_computation.10 | convolution fusion | flops 3225681920 | bytes 10490368 | tf_op jit(solution)/shard_map/dot_general | solution.py:21
  249.9 8.8 %subtract_bitcast_fusion.1 = f32[2048,512]{0,1:T(8,128)} fusion(f32[512,2048]{1,0:T(8,128)S(1)} %fusion.4, f32[512,512]{1,0:T(8,128)S(1)} %get-tuple-element.42, f32[2,2048,512]{2,1,0:T(8,128)S(1)} %bitcast.77), kind=kOutput, calls=%fused_computation.23 | convolution fusion | flops 3222274048 | bytes 13631488 | tf_op jit(solution)/shard_map/dot_general | solution.py:21
  259.4 9.8 %fusion = f32[512,2048]{1,0:T(8,128)S(1)} fusion(f32[2,2048,512]{2,1,0:T(8,128)} %param.7, f32[512,64]{1,0:T(8,128)S(1)} %get-tuple-element.25, f32[512,448]{1,0:T(8,128)S(1)} %get-tuple-element.27, f32[512,448]{1,0:T(8,128)S(1)} %get-tuple-element.26, f32[512,64]{1,0:T(8,128)S(1)} %get-tuple-element.24, s32[512]{0:T(512)S(1)} %iota_shift-right-logical_fusion, ...), kind=kOutput, calls=%fused_computation.6 | convolution fusion | flops 3225681920 | bytes 10490368 | tf_op jit(solution)/shard_map/dot_general | solution.py:21
  269.2 8.6 %subtract_bitcast_fusion = f32[2048,512]{0,1:T(8,128)} fusion(f32[512,2048]{1,0:T(8,128)S(1)} %fusion, f32[512,512]{1,0:T(8,128)S(1)} %get-tuple-element.43, f32[2,2048,512]{2,1,0:T(8,128)S(1)} %bitcast.79), kind=kOutput, calls=%fused_computation.22 | convolution fusion | flops 3222274048 | bytes 13631488 | tf_op jit(solution)/shard_map/dot_general | solution.py:21
  278.9 55.3 %reduce-scatter.3.cloned.1.call-done = f32[2048,128]{0,1:T(8,128)} async-done(((f32[2048,512]{0,1:T(8,128)}), f32[2048,128]{0,1:T(8,128)}) %reduce-scatter.3.cloned.1.call-update) | async-done | bytes 1048592 | tf_op jit(solution)/shard_map/reduce_scatter | solution.py:72
  334.2 79.5 %reduce-scatter.5.cloned.1.call-done = f32[2048,128]{0,1:T(8,128)} async-done(((f32[2048,512]{0,1:T(8,128)}), f32[2048,128]{0,1:T(8,128)}) %reduce-scatter.5.cloned.1.call-update) | async-done | bytes 1048592 | tf_op jit(solution)/shard_map/reduce_scatter | solution.py:72
  413.7 2.0 fusion.67
  416.0 1.2 fusion.29
  417.1 1.8 copy.10
  (75 shorter events, 3.1 us)
Async XLA Ops:
  6.5 229.4 %copy-start = (f32[2048]{0:T(1024)S(1)}, f32[2048]{0:T(1024)}, u32[]{:S(2)}) copy-start(f32[2048]{0:T(1024)} %param.9) | copy-start | bytes 24580
  6.5 90.4 %all-gather.5.cloned.1.call-start = ((), (), s32[]{:S(2)}) async-start(), calls=%async_computation.4 | async-start | bytes 5242880 | tf_op jit(solution)/shard_map/all_gather | solution.py:68
  13.3 164.4 %all-gather.3.cloned.1.call-start = ((), (), s32[]{:S(2)}) async-start(), calls=%async_computation.2 | async-start | bytes 5242880 | tf_op jit(solution)/shard_map/all_gather | solution.py:68
  14.4 319.8 %reduce-scatter.3.cloned.1.call-start = ((), (), s32[]{:S(2)}) async-start(), calls=%async_computation.3 | async-start | bytes 5242880 | tf_op jit(solution)/shard_map/reduce_scatter | solution.py:72
  177.7 7.2 %copy-start.3 = (f32[2048,512]{0,1:T(8,128)S(1)}, f32[2048,512]{0,1:T(8,128)}, u32[]{:S(2)}) copy-start(f32[2048,512]{0,1:T(8,128)} %all-gather.5.cloned.1.call-done) | copy-start | bytes 12582916
  177.7 7.2 %copy-start.5 = (f32[512,448]{1,0:T(8,128)S(1)}, f32[512,448]{1,0:T(8,128)}, u32[]{:S(2)}) copy-start(f32[512,448]{1,0:T(8,128)} %get-tuple-element.33) | copy-start | bytes 2752516
  177.7 7.2 %copy-start.6 = (f32[512,64]{1,0:T(8,128)S(1)}, f32[512,64]{1,0:T(8,128)}, u32[]{:S(2)}) copy-start(f32[512,64]{1,0:T(8,128)} %get-tuple-element.31) | copy-start | bytes 393220
  184.4 1.2 copy-start.4
  184.4 8.4 %slice-start = ((s8[8388608]{0:T(1024)(128)(4,1)}), s8[4194304]{0:T(1024)(128)(4,1)S(1)}, s32[]{:S(2)}) async-start(s8[8388608]{0:T(1024)(128)(4,1)} %bitcast.74), calls=%async_computation.6 | async-start | bytes 8388608
  185.7 7.2 %slice-start.1 = ((s8[8388608]{0:T(1024)(128)(4,1)}), s8[4194304]{0:T(1024)(128)(4,1)S(1)}, s32[]{:S(2)}) async-start(s8[8388608]{0:T(1024)(128)(4,1)} %bitcast.74), calls=%async_computation.7 | async-start | bytes 8388608
  185.7 7.2 %copy-start.2 = (f32[2048,512]{0,1:T(8,128)S(1)}, f32[2048,512]{0,1:T(8,128)}, u32[]{:S(2)}) copy-start(f32[2048,512]{0,1:T(8,128)} %all-gather.3.cloned.1.call-done) | copy-start | bytes 12582916
  192.8 7.3 %collective-permute-start.6 = (f32[256,512]{1,0:T(8,128)}, f32[256,512]{1,0:T(8,128)}, u32[]{:S(2)}, u32[]{:S(2)}) collective-permute-start(f32[256,512]{1,0:T(8,128)} %constant_dynamic-slice_fusion.2), channel_id=1, source_target_pairs={{0,4},{4,0},{8,12},{12,8},{16,20},{20,16},{24,28},{28,24},{1,5},{5... | collective-permute-start | bytes 1572872 | tf_op jit(solution)/shard_map/ppermute | solution.py:43
  199.6 3.2 collective-permute-start
  201.3 9.2 %collective-permute-start.7 = (f32[128,512]{1,0:T(8,128)S(1)}, f32[128,512]{1,0:T(8,128)S(1)}, u32[]{:S(2)}, u32[]{:S(2)}) collective-permute-start(f32[128,512]{1,0:T(8,128)S(1)} %constant_dynamic-slice_fusion.1), channel_id=1, source_target_pairs={{0,8},{4,12},{8,0},{12,4},{16,24},{20,28},{24,16},{28,20},{1,9},{5... | collective-permute-start | bytes 786440 | tf_op jit(solution)/shard_map/ppermute | solution.py:43
  204.1 11.1 %collective-permute-start.1 = (f32[128,512]{1,0:T(8,128)S(1)}, f32[128,512]{1,0:T(8,128)S(1)}, u32[]{:S(2)}, u32[]{:S(2)}) collective-permute-start(f32[128,512]{1,0:T(8,128)S(1)} %constant_dynamic-slice_fusion.4), channel_id=1, source_target_pairs={{0,8},{4,12},{8,0},{12,4},{16,24},{20,28},{24,16},{28,20},{1,9},{5... | collective-permute-start | bytes 786440 | tf_op jit(solution)/shard_map/ppermute | solution.py:43
  210.5 25.4 %copy-start.7 = (s32[4]{0:T(128)S(1)}, s32[4]{0:T(128)}, u32[]{:S(2)}) copy-start(s32[4]{0:T(128)} %param.10) | copy-start | bytes 52
  210.6 6.2 %collective-permute-start.8 = (f32[64,512]{1,0:T(8,128)S(1)}, f32[64,512]{1,0:T(8,128)S(1)}, u32[]{:S(2)}, u32[]{:S(2)}) collective-permute-start(f32[64,512]{1,0:T(8,128)S(1)} %constant_dynamic-slice_fusion), channel_id=1, source_target_pairs={{0,16},{4,20},{8,24},{12,28},{16,0},{20,4},{24,8},{28,12},{1,17},{... | collective-permute-start | bytes 393224 | tf_op jit(solution)/shard_map/ppermute | solution.py:43
  215.2 6.3 %collective-permute-start.2 = (f32[64,512]{1,0:T(8,128)S(1)}, f32[64,512]{1,0:T(8,128)S(1)}, u32[]{:S(2)}, u32[]{:S(2)}) collective-permute-start(f32[64,512]{1,0:T(8,128)S(1)} %constant_dynamic-slice_fusion.3), channel_id=1, source_target_pairs={{0,16},{4,20},{8,24},{12,28},{16,0},{20,4},{24,8},{28,12},{1,17},{... | collective-permute-start | bytes 393224 | tf_op jit(solution)/shard_map/ppermute | solution.py:43
  216.8 7.3 %collective-permute-start.9 = (f32[64,512]{1,0:T(8,128)S(1)}, f32[64,512]{1,0:T(8,128)S(1)}, u32[]{:S(2)}, u32[]{:S(2)}) collective-permute-start(f32[64,512]{1,0:T(8,128)S(1)} %dynamic-slice_add_fusion.4), channel_id=1, source_target_pairs={{0,16},{4,20},{8,24},{12,28},{16,0},{20,4},{24,8},{28,12},{1,17},{... | collective-permute-start | bytes 393224 | tf_op jit(solution)/shard_map/ppermute | solution.py:46
  221.6 5.0 %collective-permute-start.3 = (f32[64,512]{1,0:T(8,128)S(1)}, f32[64,512]{1,0:T(8,128)S(1)}, u32[]{:S(2)}, u32[]{:S(2)}) collective-permute-start(f32[64,512]{1,0:T(8,128)S(1)} %dynamic-slice_add_fusion.5), channel_id=1, source_target_pairs={{0,16},{4,20},{8,24},{12,28},{16,0},{20,4},{24,8},{28,12},{1,17},{... | collective-permute-start | bytes 393224 | tf_op jit(solution)/shard_map/ppermute | solution.py:46
  224.1 8.1 %collective-permute-start.10 = (f32[128,512]{1,0:T(8,128)S(1)}, f32[128,512]{1,0:T(8,128)S(1)}, u32[]{:S(2)}, u32[]{:S(2)}) collective-permute-start(f32[128,512]{1,0:T(8,128)S(1)} %pad_maximum_fusion.5), channel_id=1, source_target_pairs={{0,8},{4,12},{8,0},{12,4},{16,24},{20,28},{24,16},{28,20},{1,9},{5... | collective-permute-start | bytes 786440 | tf_op jit(solution)/shard_map/ppermute | solution.py:46
  226.7 8.3 %collective-permute-start.4 = (f32[128,512]{1,0:T(8,128)S(1)}, f32[128,512]{1,0:T(8,128)S(1)}, u32[]{:S(2)}, u32[]{:S(2)}) collective-permute-start(f32[128,512]{1,0:T(8,128)S(1)} %pad_maximum_fusion.4), channel_id=1, source_target_pairs={{0,8},{4,12},{8,0},{12,4},{16,24},{20,28},{24,16},{28,20},{1,9},{5... | collective-permute-start | bytes 786440 | tf_op jit(solution)/shard_map/ppermute | solution.py:46
  233.1 3.0 collective-permute-start.11
  235.9 2.3 collective-permute-start.5
  239.5 10.4 %slice-start.2 = ((s8[8388608]{0:T(1024)(128)(4,1)}), s8[4194304]{0:T(1024)(128)(4,1)S(1)}, s32[]{:S(2)}) async-start(s8[8388608]{0:T(1024)(128)(4,1)} %bitcast.76), calls=%async_computation.8 | async-start | bytes 8388608
  240.1 9.9 %slice-start.3 = ((s8[8388608]{0:T(1024)(128)(4,1)}), s8[4194304]{0:T(1024)(128)(4,1)S(1)}, s32[]{:S(2)}) async-start(s8[8388608]{0:T(1024)(128)(4,1)} %bitcast.76), calls=%async_computation.9 | async-start | bytes 8388608
  258.8 154.9 %reduce-scatter.5.cloned.1.call-start = ((), (), s32[]{:S(2)}) async-start(), calls=%async_computation.5 | async-start | bytes 5242880 | tf_op jit(solution)/shard_map/reduce_scatter | solution.py:72
  259.0 10.2 %slice-start.4 = ((s8[8388608]{0:T(1024)(128)(4,1)}), s8[4194304]{0:T(1024)(128)(4,1)S(1)}, s32[]{:S(2)}) async-start(s8[8388608]{0:T(1024)(128)(4,1)} %bitcast.78), calls=%async_computation.10 | async-start | bytes 8388608
  259.4 9.8 %slice-start.5 = ((s8[8388608]{0:T(1024)(128)(4,1)}), s8[4194304]{0:T(1024)(128)(4,1)S(1)}, s32[]{:S(2)}) async-start(s8[8388608]{0:T(1024)(128)(4,1)} %bitcast.78), calls=%async_computation.11 | async-start | bytes 8388608
  415.9 3.1 copy-start.1
Sparse Core Ops, SparseCore 0:
  13.4 83.4 all-gather.4
  98.5 79.2 all-gather.2
  258.9 75.2 reduce-scatter.2
  336.3 77.2 reduce-scatter.4
where the time goes:
time: 426 us; the launch traced here: 425 us
  waiting for transfers between devices  311 us (73%)
  matrix products  61.5 us (14%)
  between operations  15.9 us (4%)
  other arithmetic  13.5 us (3%)
  local copies, waits for them, and re-layouts  12.8 us (3%)
  starting transfers between devices  11.1 us (3%)
    all_gather x2, waiting for transfers between devices, per_device(): every = lax.all_gather(own, 'ba', axis=1, tiled=True)  154 us
    reduce_scatter x2, waiting for transfers between devices, per_device(): share = lax.psum_scatter(correction, 'ba', scatter_dimension=1, tiled=True)  135 us
    dot_general x5, matrix products, mdot(): jnp.dot(left, right, precision=lax.Precision.HIGH, preferred_element_type...  37.1 us
    dot_general x4, matrix products, tdot(): lax.dot_general(left, right, (((0,), (0,)), ((), ())), precision=lax.Prec...  24.3 us
    ppermute x6, waiting for transfers between devices, sum_over(): block = kept + lax.ppermute(sent, axis, [(i, i ^ bit) for i in range(size)])  12.9 us
    ppermute x6, waiting for transfers between devices, sum_over(): other = lax.ppermute(block, axis, [(i, i ^ bit) for i in range(size)])  8.74 us
  transfers between devices with their start and end apart: 16, of which 12 were waited for; matrix products, arithmetic and copies ran while one was open for 10% of the time, Pallas kernels for 0%

commit v1 on v0

--- a/solution.py
+++ b/solution.py
@@ -65,7 +65,14 @@
     for chunk in range(CHUNKS):
         columns = slice(chunk * width, (chunk + 1) * width)
         own = jnp.concatenate([aligned[0, :, columns], aligned[1, :, columns]], axis=1)
-        every = lax.all_gather(own, "ba", axis=1, tiled=True)
+        ring = [own]
+        for hop in range(3):
+            ring.append(lax.ppermute(ring[-1], "ba", [(dev, (dev + 1) % 4) for dev in range(4)]))
+        every = jnp.roll(
+            jnp.concatenate(ring[::-1], axis=1),
+            (lax.axis_index("ba") + 1) * ring[0].shape[1],
+            axis=1,
+        )
         block = tdot(psi[0], every) + turned(tdot(psi[1], every), width)
         weighted = sum_over(block, "ga", size) * local_weight[:, None]
         correction = mdot(psi[0], weighted) - mdot(psi[1], turned(weighted, width))

time: 426 us -> 408 us (0.958)
  waiting for transfers between devices: 311 us -> 289 us
  matrix products: 61.5 us -> 54 us
  starting transfers between devices: 11.1 us -> 16.3 us
  local copies, waits for them, and re-layouts: 12.8 us -> 17.9 us
    all_gather x2 -> x0, waiting for transfers between devices: 154 us -> none  [per_device(): every = lax.all_gather(own, 'ba', axis=1, tiled=True)]
    ppermute x0 -> x6, waiting for transfers between devices: none -> 131 us  [per_device(): lax.ppermute(ring[-1], 'ba', [(dev, (dev + 1) % 4) for dev in range(4)])]
    unnamed x29 -> x38, local copies, waits for them, and re-layouts: 2.65 us -> 10.6 us
    dot_general x4, matrix products: 24.3 us -> 16.4 us  [tdot(): lax.dot_general(left, right, (((0,), (0,)), ((), ())), precision=lax.Prec...]
    ppermute x0 -> x6, starting transfers between devices: none -> 5.02 us  [per_device(): lax.ppermute(ring[-1], 'ba', [(dev, (dev + 1) % 4) for dev in range(4)])]
  transfers between devices with their start and end apart: 16 -> 20, of which waited for: 12 -> 16; matrix products, arithmetic and copies ran while one was open for 10% -> 8% of each run, Pallas kernels for 0% -> 0%
where the time goes in v1:
time: 408 us; the launch traced here: 405 us
  waiting for transfers between devices  289 us (71%)
  matrix products  54 us (13%)
  local copies, waits for them, and re-layouts  17.9 us (4%)
  between operations  16.5 us (4%)
  starting transfers between devices  16.3 us (4%)
  other arithmetic  10.9 us (3%)
    reduce_scatter x2, waiting for transfers between devices, per_device(): share = lax.psum_scatter(correction, 'ba', scatter_dimension=1, tiled=True)  135 us
    ppermute x6, waiting for transfers between devices, per_device(): lax.ppermute(ring[-1], 'ba', [(dev, (dev + 1) % 4) for dev in range(4)])  131 us
    dot_general x5, matrix products, mdot(): jnp.dot(left, right, precision=lax.Precision.HIGH, preferred_element_type...  37.6 us
    dot_general x4, matrix products, tdot(): lax.dot_general(left, right, (((0,), (0,)), ((), ())), precision=lax.Prec...  16.4 us
    ppermute x6, waiting for transfers between devices, sum_over(): block = kept + lax.ppermute(sent, axis, [(i, i ^ bit) for i in range(size)])  12.9 us
    unnamed x38, local copies, waits for them, and re-layouts  10.6 us
    ppermute x6, waiting for transfers between devices, sum_over(): other = lax.ppermute(block, axis, [(i, i ^ bit) for i in range(size)])  9.51 us
  transfers between devices with their start and end apart: 20, of which 16 were waited for; matrix products, arithmetic and copies ran while one was open for 8% of the time, Pallas kernels for 0%

profile of v1, /device:TPU:0, one launch (start us, length us, event | category | flops | bytes accessed | tf_op | source)
XLA Modules:
  0.0 404.8 jit_solution(10407844076826920977)
XLA Ops:
  6.5 1.2 dynamic_slice.45
  8.9 2.9 copy.6
  11.8 2.8 fusion.33
  15.7 3.1 collective-permute-start
  18.9 1.6 collective-permute-start.9
  20.5 24.3 %collective-permute-done = f32[2048,128]{0,1:T(8,128)S(1)} collective-permute-done((f32[2048,128]{0,1:T(8,128)S(1)}, f32[2048,128]{0,1:T(8,128)S(1)}, u32[]{:S(2)}, u32[]{:S(2)}) %collective-permute-start) | collective-permute-done | bytes 1048608 | tf_op jit(solution)/shard_map/ppermute | solution.py:70
  44.8 1.0 copy-done.6
  45.8 21.6 %collective-permute-done.9 = f32[2048,128]{0,1:T(8,128)} collective-permute-done((f32[2048,128]{0,1:T(8,128)S(1)}, f32[2048,128]{0,1:T(8,128)}, u32[]{:S(2)}, u32[]{:S(2)}) %collective-permute-start.9) | collective-permute-done | bytes 1048608 | tf_op jit(solution)/shard_map/ppermute | solution.py:70
  67.4 22.5 %collective-permute-done.1 = f32[2048,128]{0,1:T(8,128)} collective-permute-done((f32[2048,128]{0,1:T(8,128)S(1)}, f32[2048,128]{0,1:T(8,128)}, u32[]{:S(2)}, u32[]{:S(2)}) %collective-permute-start.1) | collective-permute-done | bytes 1048608 | tf_op jit(solution)/shard_map/ppermute | solution.py:70
  89.9 22.5 %collective-permute-done.10 = f32[2048,128]{0,1:T(8,128)} collective-permute-done((f32[2048,128]{0,1:T(8,128)}, f32[2048,128]{0,1:T(8,128)}, u32[]{:S(2)}, u32[]{:S(2)}) %collective-permute-start.10) | collective-permute-done | bytes 1048608 | tf_op jit(solution)/shard_map/ppermute | solution.py:70
  112.6 22.2 %collective-permute-done.2 = f32[2048,128]{0,1:T(8,128)} collective-permute-done((f32[2048,128]{0,1:T(8,128)}, f32[2048,128]{0,1:T(8,128)}, u32[]{:S(2)}, u32[]{:S(2)}) %collective-permute-start.2) | collective-permute-done | bytes 1048608 | tf_op jit(solution)/shard_map/ppermute | solution.py:70
  134.8 1.4 constant_dynamic-update-slice_fusion.4
  136.2 1.4 constant_dynamic-update-slice_fusion.3
  137.8 18.5 %collective-permute-done.11 = f32[2048,128]{0,1:T(8,128)S(1)} collective-permute-done((f32[2048,128]{0,1:T(8,128)}, f32[2048,128]{0,1:T(8,128)S(1)}, u32[]{:S(2)}, u32[]{:S(2)}) %collective-permute-start.11) | collective-permute-done | bytes 1048608 | tf_op jit(solution)/shard_map/ppermute | solution.py:70
  156.3 1.4 constant_dynamic-update-slice_fusion.8
  157.8 1.4 constant_dynamic-update-slice_fusion.7
  159.4 3.8 fusion.40
  163.8 3.8 fusion.43
  168.1 4.6 %fusion.49 = f32[512,512]{1,0:T(8,128)S(1)} fusion(f32[2,2048,512]{2,1,0:T(8,128)S(1)} %bitcast.79, f32[512,64]{1,0:T(8,128)S(1)} %get-tuple-element.26, f32[512,448]{1,0:T(8,128)S(1)} %get-tuple-element.28, f32[512,448]{1,0:T(8,128)S(1)} %get-tuple-element.27, f32[512,64]{1,0:T(8,128)S(1)} %get-tuple-element.25, s32[]{:T(128)S(6)} %select_n.238, ...), kind=kOutput, calls=%fused_computation.52 | convolution fusion | flops 3226992640 | bytes 12063236 | tf_op jit(solution)/shard_map/dot_general | solution.py:11
  172.8 0.8 constant_dynamic-slice_fusion.5
  173.6 4.1 %fusion.46 = f32[512,512]{1,0:T(8,128)S(1)} fusion(f32[2,2048,512]{2,1,0:T(8,128)S(1)} %bitcast.79, f32[512,64]{1,0:T(8,128)S(1)} %get-tuple-element.36, f32[512,448]{1,0:T(8,128)S(1)} %get-tuple-element.38, f32[512,448]{1,0:T(8,128)S(1)} %get-tuple-element.37, f32[512,64]{1,0:T(8,128)S(1)} %get-tuple-element.35, s32[]{:T(128)S(6)} %select_n.238, ...), kind=kOutput, calls=%fused_computation.51 | convolution fusion | flops 3226992640 | bytes 12063236 | tf_op jit(solution)/shard_map/dot_general | solution.py:11
  177.7 0.8 constant_dynamic-slice_fusion.2
  179.1 1.2 dynamic-slice_add_fusion.1
  180.2 1.6 collective-permute-start.4
  181.8 1.2 dynamic-slice_add_fusion
  183.7 5.8 %collective-permute-done.4 = f32[128,512]{1,0:T(8,128)S(1)} collective-permute-done((f32[128,512]{1,0:T(8,128)S(1)}, f32[128,512]{1,0:T(8,128)S(1)}, u32[]{:S(2)}, u32[]{:S(2)}) %collective-permute-start.4) | collective-permute-done | bytes 262176 | tf_op jit(solution)/shard_map/ppermute | solution.py:43
  189.6 1.6 collective-permute-start.5
  191.2 3.0 collective-permute-done.13
  194.2 1.6 collective-permute-start.14
  196.4 4.1 %collective-permute-done.14 = f32[64,512]{1,0:T(8,128)S(1)} collective-permute-done((f32[64,512]{1,0:T(8,128)S(1)}, f32[64,512]{1,0:T(8,128)S(1)}, u32[]{:S(2)}, u32[]{:S(2)}) %collective-permute-start.14) | collective-permute-done | bytes 131104 | tf_op jit(solution)/shard_map/ppermute | solution.py:43
  200.6 1.6 collective-permute-start.15
  202.2 0.9 collective-permute-done.6
  203.1 1.6 collective-permute-start.7
  204.7 0.9 collective-permute-done.15
  205.6 1.6 collective-permute-start.16
  207.2 4.0 collective-permute-done.7
  212.1 1.9 collective-permute-done.16
  214.0 0.9 pad_maximum_fusion.3
  215.2 1.8 collective-permute-done.17
  217.9 10.0 %fusion.2 = f32[512,2048]{1,0:T(8,128)S(1)} fusion(f32[2,2048,512]{2,1,0:T(8,128)} %param.9, f32[512,64]{1,0:T(8,128)S(1)} %get-tuple-element.30, f32[512,448]{1,0:T(8,128)S(1)} %get-tuple-element.32, f32[512,448]{1,0:T(8,128)S(1)} %get-tuple-element.31, f32[512,64]{1,0:T(8,128)S(1)} %get-tuple-element.29, s32[512]{0:T(512)S(1)} %iota_shift-right-logical_fusion, ...), kind=kOutput, calls=%fused_computation.12 | convolution fusion | flops 3225681920 | bytes 10490368 | tf_op jit(solution)/shard_map/dot_general | solution.py:21
  227.9 8.6 %subtract_bitcast_fusion = f32[2048,512]{0,1:T(8,128)} fusion(f32[512,2048]{1,0:T(8,128)S(1)} %fusion.2, f32[512,512]{1,0:T(8,128)S(1)} %get-tuple-element.48, f32[2,2048,512]{2,1,0:T(8,128)S(1)} %bitcast.81), kind=kOutput, calls=%fused_computation.28 | convolution fusion | flops 3222274048 | bytes 13631488 | tf_op jit(solution)/shard_map/dot_general | solution.py:21
  237.1 10.1 %fusion.6 = f32[512,2048]{1,0:T(8,128)S(1)} fusion(f32[2,2048,512]{2,1,0:T(8,128)} %param.9, f32[512,64]{1,0:T(8,128)S(1)} %get-tuple-element.20, f32[512,448]{1,0:T(8,128)S(1)} %get-tuple-element.22, f32[512,448]{1,0:T(8,128)S(1)} %get-tuple-element.21, f32[512,64]{1,0:T(8,128)S(1)} %get-tuple-element.19, s32[512]{0:T(512)S(1)} %iota_shift-right-logical_fusion, ...), kind=kOutput, calls=%fused_computation.16 | convolution fusion | flops 3225681920 | bytes 10490368 | tf_op jit(solution)/shard_map/dot_general | solution.py:21
  247.3 8.7 %subtract_bitcast_fusion.1 = f32[2048,512]{0,1:T(8,128)} fusion(f32[512,2048]{1,0:T(8,128)S(1)} %fusion.6, f32[512,512]{1,0:T(8,128)S(1)} %get-tuple-element.47, f32[2,2048,512]{2,1,0:T(8,128)S(1)} %bitcast.83), kind=kOutput, calls=%fused_computation.29 | convolution fusion | flops 3222274048 | bytes 13631488 | tf_op jit(solution)/shard_map/dot_general | solution.py:21
  257.2 55.7 %reduce-scatter.5.cloned.1.call-done = f32[2048,128]{0,1:T(8,128)} async-done(((f32[2048,512]{0,1:T(8,128)}), f32[2048,128]{0,1:T(8,128)}) %reduce-scatter.5.cloned.1.call-update) | async-done | bytes 1048592 | tf_op jit(solution)/shard_map/reduce_scatter | solution.py:79
  312.9 79.6 %reduce-scatter.3.cloned.1.call-done = f32[2048,128]{0,1:T(8,128)} async-done(((f32[2048,512]{0,1:T(8,128)}), f32[2048,128]{0,1:T(8,128)}) %reduce-scatter.3.cloned.1.call-update) | async-done | bytes 1048592 | tf_op jit(solution)/shard_map/reduce_scatter | solution.py:79
  392.5 2.0 fusion.81
  394.8 1.2 fusion.31
  396.0 1.8 copy.10
  (91 shorter events, 7.7 us)
Async XLA Ops:
  6.5 208.4 %copy-start = (f32[2048]{0:T(1024)S(1)}, f32[2048]{0:T(1024)}, u32[]{:S(2)}) copy-start(f32[2048]{0:T(1024)} %param.11) | copy-start | bytes 24580
  6.5 306.3 %reduce-scatter.5.cloned.1.call-start = ((), (), s32[]{:S(2)}) async-start(), calls=%async_computation.3 | async-start | bytes 5242880 | tf_op jit(solution)/shard_map/reduce_scatter | solution.py:79
  14.8 0.8 copy-start.2
  14.8 4.0 copy-start.4
  15.7 29.1 %collective-permute-start = (f32[2048,128]{0,1:T(8,128)S(1)}, f32[2048,128]{0,1:T(8,128)S(1)}, u32[]{:S(2)}, u32[]{:S(2)}) collective-permute-start(f32[2048,128]{0,1:T(8,128)S(1)} %pad_maximum_fusion), channel_id=1, source_target_pairs={{0,1},{1,2},{2,3},{3,0},{4,5},{5,6},{6,7},{7,4},{8,9},{9,10},{10,1... | collective-permute-start | bytes 3145736 | tf_op jit(solution)/shard_map/ppermute | solution.py:70
  18.9 48.5 %collective-permute-start.9 = (f32[2048,128]{0,1:T(8,128)S(1)}, f32[2048,128]{0,1:T(8,128)}, u32[]{:S(2)}, u32[]{:S(2)}) collective-permute-start(f32[2048,128]{0,1:T(8,128)S(1)} %pad_maximum_fusion.1), channel_id=1, source_target_pairs={{0,1},{1,2},{2,3},{3,0},{4,5},{5,6},{6,7},{7,4},{8,9},{9,10},{10,1... | collective-permute-start | bytes 3145736 | tf_op jit(solution)/shard_map/ppermute | solution.py:70
  44.8 1.0 copy-start.6
  45.8 44.1 %collective-permute-start.1 = (f32[2048,128]{0,1:T(8,128)S(1)}, f32[2048,128]{0,1:T(8,128)}, u32[]{:S(2)}, u32[]{:S(2)}) collective-permute-start(f32[2048,128]{0,1:T(8,128)S(1)} %collective-permute-done), channel_id=1, source_target_pairs={{0,1},{1,2},{2,3},{3,0},{4,5},{5,6},{6,7},{7,4},{8,9},{9,10},{10,1... | collective-permute-start | bytes 3145736 | tf_op jit(solution)/shard_map/ppermute | solution.py:70
  67.4 44.9 %collective-permute-start.10 = (f32[2048,128]{0,1:T(8,128)}, f32[2048,128]{0,1:T(8,128)}, u32[]{:S(2)}, u32[]{:S(2)}) collective-permute-start(f32[2048,128]{0,1:T(8,128)} %collective-permute-done.9), channel_id=1, source_target_pairs={{0,1},{1,2},{2,3},{3,0},{4,5},{5,6},{6,7},{7,4},{8,9},{9,10},{10,1... | collective-permute-start | bytes 3145736 | tf_op jit(solution)/shard_map/ppermute | solution.py:70
  89.9 44.9 %collective-permute-start.2 = (f32[2048,128]{0,1:T(8,128)}, f32[2048,128]{0,1:T(8,128)}, u32[]{:S(2)}, u32[]{:S(2)}) collective-permute-start(f32[2048,128]{0,1:T(8,128)} %collective-permute-done.1), channel_id=1, source_target_pairs={{0,1},{1,2},{2,3},{3,0},{4,5},{5,6},{6,7},{7,4},{8,9},{9,10},{10,1... | collective-permute-start | bytes 3145736 | tf_op jit(solution)/shard_map/ppermute | solution.py:70
  89.9 47.8 %copy-start.7 = (f32[2048,128]{0,1:T(8,128)S(1)}, f32[2048,128]{0,1:T(8,128)}, u32[]{:S(2)}) copy-start(f32[2048,128]{0,1:T(8,128)} %copy-done.6) | copy-start | bytes 3145732
  112.3 43.9 %collective-permute-start.11 = (f32[2048,128]{0,1:T(8,128)}, f32[2048,128]{0,1:T(8,128)S(1)}, u32[]{:S(2)}, u32[]{:S(2)}) collective-permute-start(f32[2048,128]{0,1:T(8,128)} %collective-permute-done.10), channel_id=1, source_target_pairs={{0,1},{1,2},{2,3},{3,0},{4,5},{5,6},{6,7},{7,4},{8,9},{9,10},{10,1... | collective-permute-start | bytes 3145736 | tf_op jit(solution)/shard_map/ppermute | solution.py:70
  134.8 24.6 %slice-start = ((s8[8388608]{0:T(1024)(128)(4,1)}), s8[4194304]{0:T(1024)(128)(4,1)S(1)}, s32[]{:S(2)}) async-start(s8[8388608]{0:T(1024)(128)(4,1)} %bitcast.78), calls=%async_computation.4 | async-start | bytes 8388608
  156.3 3.1 slice-start.1
  173.6 5.5 %collective-permute-start.3 = (f32[256,512]{1,0:T(8,128)}, f32[256,512]{1,0:T(8,128)}, u32[]{:S(2)}, u32[]{:S(2)}) collective-permute-start(f32[256,512]{1,0:T(8,128)} %constant_dynamic-slice_fusion.5), channel_id=1, source_target_pairs={{0,4},{4,0},{8,12},{12,8},{16,20},{20,16},{24,28},{28,24},{1,5},{5... | collective-permute-start | bytes 1572872 | tf_op jit(solution)/shard_map/ppermute | solution.py:43
  178.6 3.3 collective-permute-start.12
  180.2 9.2 %collective-permute-start.4 = (f32[128,512]{1,0:T(8,128)S(1)}, f32[128,512]{1,0:T(8,128)S(1)}, u32[]{:S(2)}, u32[]{:S(2)}) collective-permute-start(f32[128,512]{1,0:T(8,128)S(1)} %constant_dynamic-slice_fusion.4), channel_id=1, source_target_pairs={{0,8},{4,12},{8,0},{12,4},{16,24},{20,28},{24,16},{28,20},{1,9},{5... | collective-permute-start | bytes 786440 | tf_op jit(solution)/shard_map/ppermute | solution.py:43
  183.0 11.1 %collective-permute-start.13 = (f32[128,512]{1,0:T(8,128)S(1)}, f32[128,512]{1,0:T(8,128)S(1)}, u32[]{:S(2)}, u32[]{:S(2)}) collective-permute-start(f32[128,512]{1,0:T(8,128)S(1)} %constant_dynamic-slice_fusion.1), channel_id=1, source_target_pairs={{0,8},{4,12},{8,0},{12,4},{16,24},{20,28},{24,16},{28,20},{1,9},{5... | collective-permute-start | bytes 786440 | tf_op jit(solution)/shard_map/ppermute | solution.py:43
  189.5 25.4 %copy-start.8 = (s32[4]{0:T(128)S(1)}, s32[4]{0:T(128)}, u32[]{:S(2)}) copy-start(s32[4]{0:T(128)} %param.12) | copy-start | bytes 52
  189.6 6.3 %collective-permute-start.5 = (f32[64,512]{1,0:T(8,128)S(1)}, f32[64,512]{1,0:T(8,128)S(1)}, u32[]{:S(2)}, u32[]{:S(2)}) collective-permute-start(f32[64,512]{1,0:T(8,128)S(1)} %constant_dynamic-slice_fusion.3), channel_id=1, source_target_pairs={{0,16},{4,20},{8,24},{12,28},{16,0},{20,4},{24,8},{28,12},{1,17},{... | collective-permute-start | bytes 393224 | tf_op jit(solution)/shard_map/ppermute | solution.py:43
  194.2 6.3 %collective-permute-start.14 = (f32[64,512]{1,0:T(8,128)S(1)}, f32[64,512]{1,0:T(8,128)S(1)}, u32[]{:S(2)}, u32[]{:S(2)}) collective-permute-start(f32[64,512]{1,0:T(8,128)S(1)} %constant_dynamic-slice_fusion), channel_id=1, source_target_pairs={{0,16},{4,20},{8,24},{12,28},{16,0},{20,4},{24,8},{28,12},{1,17},{... | collective-permute-start | bytes 393224 | tf_op jit(solution)/shard_map/ppermute | solution.py:43
  195.8 7.2 %collective-permute-start.6 = (f32[64,512]{1,0:T(8,128)S(1)}, f32[64,512]{1,0:T(8,128)S(1)}, u32[]{:S(2)}, u32[]{:S(2)}) collective-permute-start(f32[64,512]{1,0:T(8,128)S(1)} %dynamic-slice_add_fusion.5), channel_id=1, source_target_pairs={{0,16},{4,20},{8,24},{12,28},{16,0},{20,4},{24,8},{28,12},{1,17},{... | collective-permute-start | bytes 393224 | tf_op jit(solution)/shard_map/ppermute | solution.py:46
  200.6 5.0 %collective-permute-start.15 = (f32[64,512]{1,0:T(8,128)S(1)}, f32[64,512]{1,0:T(8,128)S(1)}, u32[]{:S(2)}, u32[]{:S(2)}) collective-permute-start(f32[64,512]{1,0:T(8,128)S(1)} %dynamic-slice_add_fusion.4), channel_id=1, source_target_pairs={{0,16},{4,20},{8,24},{12,28},{16,0},{20,4},{24,8},{28,12},{1,17},{... | collective-permute-start | bytes 393224 | tf_op jit(solution)/shard_map/ppermute | solution.py:46
  203.1 8.1 %collective-permute-start.7 = (f32[128,512]{1,0:T(8,128)S(1)}, f32[128,512]{1,0:T(8,128)S(1)}, u32[]{:S(2)}, u32[]{:S(2)}) collective-permute-start(f32[128,512]{1,0:T(8,128)S(1)} %pad_maximum_fusion.4), channel_id=1, source_target_pairs={{0,8},{4,12},{8,0},{12,4},{16,24},{20,28},{24,16},{28,20},{1,9},{5... | collective-permute-start | bytes 786440 | tf_op jit(solution)/shard_map/ppermute | solution.py:46
  205.6 8.3 %collective-permute-start.16 = (f32[128,512]{1,0:T(8,128)S(1)}, f32[128,512]{1,0:T(8,128)S(1)}, u32[]{:S(2)}, u32[]{:S(2)}) collective-permute-start(f32[128,512]{1,0:T(8,128)S(1)} %pad_maximum_fusion.5), channel_id=1, source_target_pairs={{0,8},{4,12},{8,0},{12,4},{16,24},{20,28},{24,16},{28,20},{1,9},{5... | collective-permute-start | bytes 786440 | tf_op jit(solution)/shard_map/ppermute | solution.py:46
  212.1 3.0 collective-permute-start.8
  214.9 2.1 collective-permute-start.17
  217.5 10.4 %slice-start.2 = ((s8[8388608]{0:T(1024)(128)(4,1)}), s8[4194304]{0:T(1024)(128)(4,1)S(1)}, s32[]{:S(2)}) async-start(s8[8388608]{0:T(1024)(128)(4,1)} %bitcast.80), calls=%async_computation.6 | async-start | bytes 8388608
  217.8 10.0 %slice-start.3 = ((s8[8388608]{0:T(1024)(128)(4,1)}), s8[4194304]{0:T(1024)(128)(4,1)S(1)}, s32[]{:S(2)}) async-start(s8[8388608]{0:T(1024)(128)(4,1)} %bitcast.80), calls=%async_computation.7 | async-start | bytes 8388608
  236.5 155.9 %reduce-scatter.3.cloned.1.call-start = ((), (), s32[]{:S(2)}) async-start(), calls=%async_computation.2 | async-start | bytes 5242880 | tf_op jit(solution)/shard_map/reduce_scatter | solution.py:79
  236.7 10.5 %slice-start.4 = ((s8[8388608]{0:T(1024)(128)(4,1)}), s8[4194304]{0:T(1024)(128)(4,1)S(1)}, s32[]{:S(2)}) async-start(s8[8388608]{0:T(1024)(128)(4,1)} %bitcast.82), calls=%async_computation.8 | async-start | bytes 8388608
  237.1 10.1 %slice-start.5 = ((s8[8388608]{0:T(1024)(128)(4,1)}), s8[4194304]{0:T(1024)(128)(4,1)S(1)}, s32[]{:S(2)}) async-start(s8[8388608]{0:T(1024)(128)(4,1)} %bitcast.82), calls=%async_computation.9 | async-start | bytes 8388608
  255.9 136.5 %copy-start.3 = (f32[2048,64]{0,1:T(8,128)S(1)}, f32[2048,64]{0,1:T(8,128)}, u32[]{:S(2)}) copy-start(f32[2048,64]{0,1:T(8,128)} %copy-done.2) | copy-start | bytes 1572868
  255.9 136.5 %copy-start.5 = (f32[2048,64]{0,1:T(8,128)S(1)}, f32[2048,64]{0,1:T(8,128)}, u32[]{:S(2)}) copy-start(f32[2048,64]{0,1:T(8,128)} %copy-done.4) | copy-start | bytes 1572868
  394.7 3.1 copy-start.1
Sparse Core Ops, SparseCore 0:
  236.7 76.1 reduce-scatter.4
  315.1 77.2 reduce-scatter.2
